TPU v7x, 32 devices: a whole 2x2x4 slice. The times are simulated.
32 devices in a mesh: shard: 2 (over x), ctx: 4 (over y, core), tp: 4 (over z).
Axes of the slice: x: 2, y: 2, z: 4, core: 2. Of those that a mesh axis runs over, the one named last changes fastest.
Arguments:
- tokens: bfloat16 [6, 608, 1024], P('shard', 'ctx'), may hold values from -6 to 6
- pad_mask: int32 [6, 608], P('shard', 'ctx'), may hold values from 0 to 1, as said below
- ln1_gain: float32 [1024], replicated, may hold values from 0.25 to 1.75
- ln1_shift: float32 [1024], replicated, may hold values from -3 to 3
- w_qkv: bfloat16 [3, 1024, 1024], P(None, 'shard', 'tp'), may hold values from -0.1875 to 0.1875
- b_qv: float32 [2, 1024], P(None, 'tp'), may hold values from -3 to 3
- w_out: bfloat16 [1024, 1024], P('tp', 'shard'), may hold values from -1 to 1
- b_out: float32 [1024], replicated, may hold values from -3 to 3
- ln2_gain: float32 [1024], replicated, may hold values from 0.25 to 1.75
- ln2_shift: float32 [1024], replicated, may hold values from -3 to 3
- w_up: bfloat16 [1024, 4096], P('shard', 'tp'), may hold values from -0.1875 to 0.1875
- b_up: float32 [4096], P('tp'), may hold values from -3 to 3
- w_down: bfloat16 [4096, 1024], P('tp', 'shard'), may hold values from -0.09375 to 0.09375
- b_down: float32 [1024], replicated, may hold values from -4 to 4
- cotangent: bfloat16 [6, 608, 1024], P('shard', 'ctx'), may hold values from -6 to 6
Outputs:
- out_tokens: float32 [6, 608, 1024], P('shard', 'ctx')
- grad_tokens: float32 [6, 608, 1024], P('shard', 'ctx')
- grad_w_qkv: float32 [3, 1024, 1024], P(None, 'shard', 'tp')
- grad_b_qv: float32 [2, 1024], P(None, 'tp')
- grad_w_out: float32 [1024, 1024], P('tp', 'shard')
- grad_b_out: float32 [1024], replicated
- grad_ln1_gain: float32 [1024], replicated
- grad_ln1_shift: float32 [1024], replicated
- grad_ln2_gain: float32 [1024], replicated
- grad_ln2_shift: float32 [1024], replicated
- grad_w_up: float32 [1024, 4096], P('shard', 'tp')
- grad_b_up: float32 [4096], P('tp')
- grad_w_down: float32 [4096, 1024], P('tp', 'shard')
- grad_b_down: float32 [1024], replicated
Inputs may be any that keep to these rules, and one draw needn't show every extreme that they name: `pad_mask`: each image has exactly 577 ones; the 31 padding slots may lie anywhere in the image.
All inputs are finite; a program needn't handle non-finite values.
Results may differ from a plain program's by a relative error of at most 0.02.
Values may be sent and summed in bfloat16 or wider, within the bound.
A program may use at most 128 MiB of HBM per device.

v0:
```python
import math
import jax
import jax.numpy as jnp
from jax import lax
from jax.sharding import PartitionSpec as P

HD = 64
NEG_FILL = -1e30


def normalize(values, gain, shift):
    row_mean = jnp.mean(values, axis=-1, keepdims=True)
    centred = values - row_mean
    inv_std = lax.rsqrt(jnp.mean(centred * centred, axis=-1, keepdims=True) + 1e-06)
    unit_rows = centred * inv_std
    return (unit_rows, inv_std, unit_rows * gain + shift)


def norm_back(upstream, unit_rows, inv_std, gain):
    scaled = upstream * gain
    centre = jnp.mean(scaled, axis=-1, keepdims=True)
    along = jnp.mean(scaled * unit_rows, axis=-1, keepdims=True)
    return inv_std * (scaled - centre - unit_rows * along)


def gelu_slope(pre_act):
    return (
        0.5 * (1.0 + lax.erf(pre_act * 0.7071067811865476))
        + pre_act * jnp.exp(-0.5 * pre_act * pre_act) * 0.3989422804014327
    )


def body(
    tokens,
    pad_mask,
    ln1_gain,
    ln1_shift,
    w_qkv,
    b_qv,
    w_out,
    b_out,
    ln2_gain,
    ln2_shift,
    w_up,
    b_up,
    w_down,
    b_down,
    cotangent,
):
    scale = 1.0 / math.sqrt(HD)
    images, piece, width = tokens.shape
    tok_count = images * piece
    qkv_full, out_full = (
        lax.all_gather(w_qkv, "shard", axis=1, tiled=True),
        lax.all_gather(w_out, "shard", axis=1, tiled=True),
    )
    up_full, down_full = (
        lax.all_gather(w_up, "shard", axis=0, tiled=True),
        lax.all_gather(w_down, "shard", axis=1, tiled=True),
    )
    local_width = out_full.shape[0]
    local_heads = local_width // HD
    inputs_wide = tokens.reshape(tok_count, width).astype(jnp.float32)
    first_unit, first_inv, first_norm = normalize(inputs_wide, ln1_gain, ln1_shift)
    first_low = first_norm.astype(jnp.bfloat16)
    projected = jnp.einsum("td,cdh->cth", first_low, qkv_full, preferred_element_type=jnp.float32)
    queries = (projected[0] + b_qv[0]).astype(jnp.bfloat16)
    key_local = projected[1].astype(jnp.bfloat16).reshape(images, piece, local_width)
    value_local = (projected[2] + b_qv[1]).astype(jnp.bfloat16).reshape(images, piece, local_width)
    valid_local = (pad_mask > 0).astype(jnp.bfloat16)
    key_all, value_all, valid_all = (
        lax.all_gather(key_local, "ctx", axis=1, tiled=True),
        lax.all_gather(value_local, "ctx", axis=1, tiled=True),
        lax.all_gather(valid_local, "ctx", axis=1, tiled=True),
    )
    seq_len = key_all.shape[1]
    query_heads = queries.reshape(images, piece, local_heads, HD)
    key_heads = key_all.reshape(images, seq_len, local_heads, HD)
    value_heads = value_all.reshape(images, seq_len, local_heads, HD)

    def masked_scores():
        scores = (
            jnp.einsum(
                "iqhe,ikhe->ihqk", query_heads, key_heads, preferred_element_type=jnp.float32
            )
            * scale
        )
        return jnp.where(valid_all[:, None, None, :] > 0.5, scores, NEG_FILL)

    scores = masked_scores()
    row_top = jnp.max(scores, axis=-1, keepdims=True)
    log_total = row_top + jnp.log(jnp.sum(jnp.exp(scores - row_top), axis=-1, keepdims=True))
    weights_low = jnp.exp(scores - log_total).astype(jnp.bfloat16)
    attended = jnp.einsum(
        "ihqk,ikhe->iqhe", weights_low, value_heads, preferred_element_type=jnp.float32
    )
    attended = attended.astype(jnp.bfloat16).reshape(tok_count, local_width)
    attn_part = jnp.dot(attended, out_full, preferred_element_type=jnp.float32)
    middle = (
        inputs_wide + lax.psum(attn_part.astype(jnp.bfloat16), "tp").astype(jnp.float32) + b_out
    )
    second_unit, second_inv, second_norm = normalize(middle, ln2_gain, ln2_shift)
    second_low = second_norm.astype(jnp.bfloat16)
    pre_act = jnp.dot(second_low, up_full, preferred_element_type=jnp.float32) + b_up
    activated = jax.nn.gelu(pre_act, approximate=False).astype(jnp.bfloat16)
    mlp_part = jnp.dot(activated, down_full, preferred_element_type=jnp.float32)
    result = middle + lax.psum(mlp_part.astype(jnp.bfloat16), "tp").astype(jnp.float32) + b_down
    out_tokens = result.reshape(images, piece, width)
    upstream_low = cotangent.reshape(tok_count, width)
    upstream_wide = upstream_low.astype(jnp.float32)
    act_grad = jnp.dot(upstream_low, down_full.T, preferred_element_type=jnp.float32) * gelu_slope(
        pre_act
    )
    act_low = act_grad.astype(jnp.bfloat16)
    grad_down = jnp.einsum("tf,td->fd", activated, upstream_low, preferred_element_type=jnp.float32)
    grad_up = jnp.einsum("td,tf->df", second_low, act_low, preferred_element_type=jnp.float32)
    norm2_part = jnp.dot(act_low, up_full.T, preferred_element_type=jnp.float32)
    norm2_grad = lax.psum(norm2_part.astype(jnp.bfloat16), "tp").astype(jnp.float32)
    middle_grad = upstream_wide + norm_back(norm2_grad, second_unit, second_inv, ln2_gain)
    middle_low = middle_grad.astype(jnp.bfloat16)
    grad_out = jnp.einsum("th,td->hd", attended, middle_low, preferred_element_type=jnp.float32)
    attended_grad = jnp.dot(middle_low, out_full.T, preferred_element_type=jnp.float32)
    attended_grad = attended_grad.astype(jnp.bfloat16).reshape(images, piece, local_heads, HD)
    weights = jnp.exp(masked_scores() - log_total)
    weights_low = weights.astype(jnp.bfloat16)
    weight_grad = jnp.einsum(
        "iqhe,ikhe->ihqk", attended_grad, value_heads, preferred_element_type=jnp.float32
    )
    row_dot = jnp.sum(weights * weight_grad, axis=-1, keepdims=True)
    score_grad = (scale * weights * (weight_grad - row_dot)).astype(jnp.bfloat16)
    query_grad = jnp.einsum(
        "ihqk,ikhe->iqhe", score_grad, key_heads, preferred_element_type=jnp.float32
    ).reshape(tok_count, local_width)
    key_part = jnp.einsum(
        "ihqk,iqhe->ikhe", score_grad, query_heads, preferred_element_type=jnp.float32
    ).reshape(images, seq_len, local_width)
    value_part = jnp.einsum(
        "ihqk,iqhe->ikhe", weights_low, attended_grad, preferred_element_type=jnp.float32
    ).reshape(images, seq_len, local_width)
    key_grad, value_grad = (
        lax.psum_scatter(
            key_part.astype(jnp.bfloat16), "ctx", scatter_dimension=1, tiled=True
        ).astype(jnp.float32),
        lax.psum_scatter(
            value_part.astype(jnp.bfloat16), "ctx", scatter_dimension=1, tiled=True
        ).astype(jnp.float32),
    )
    key_grad = key_grad.reshape(tok_count, local_width)
    value_grad = value_grad.reshape(tok_count, local_width)
    proj_grad = jnp.stack([query_grad, key_grad, value_grad]).astype(jnp.bfloat16)
    grad_qkv = jnp.einsum("td,cth->cdh", first_low, proj_grad, preferred_element_type=jnp.float32)
    norm1_part = jnp.einsum("cth,cdh->td", proj_grad, qkv_full, preferred_element_type=jnp.float32)
    norm1_grad = lax.psum(norm1_part.astype(jnp.bfloat16), "tp").astype(jnp.float32)
    input_grad = middle_grad + norm_back(norm1_grad, first_unit, first_inv, ln1_gain)
    grad_tokens = input_grad.reshape(images, piece, width)
    small = lax.psum(
        (
            jnp.stack([jnp.sum(query_grad, axis=0), jnp.sum(value_grad, axis=0)]),
            jnp.sum(middle_grad, axis=0),
            jnp.sum(norm1_grad * first_unit, axis=0),
            jnp.sum(norm1_grad, axis=0),
            jnp.sum(norm2_grad * second_unit, axis=0),
            jnp.sum(norm2_grad, axis=0),
            jnp.sum(act_grad, axis=0),
            jnp.sum(upstream_wide, axis=0),
        ),
        ("shard", "ctx"),
    )
    summed = (
        lax.psum(grad_qkv.astype(jnp.bfloat16), "ctx").astype(jnp.float32),
        lax.psum(grad_out.astype(jnp.bfloat16), "ctx").astype(jnp.float32),
        lax.psum(grad_up.astype(jnp.bfloat16), "ctx").astype(jnp.float32),
        lax.psum(grad_down.astype(jnp.bfloat16), "ctx").astype(jnp.float32),
    )
    big_sums = (
        lax.psum_scatter(
            summed[0].astype(jnp.bfloat16), "shard", scatter_dimension=1, tiled=True
        ).astype(jnp.float32),
        lax.psum_scatter(
            summed[1].astype(jnp.bfloat16), "shard", scatter_dimension=1, tiled=True
        ).astype(jnp.float32),
        lax.psum_scatter(
            summed[2].astype(jnp.bfloat16), "shard", scatter_dimension=0, tiled=True
        ).astype(jnp.float32),
        lax.psum_scatter(
            summed[3].astype(jnp.bfloat16), "shard", scatter_dimension=1, tiled=True
        ).astype(jnp.float32),
    )
    return (
        out_tokens,
        grad_tokens,
        big_sums[0],
        small[0],
        big_sums[1],
        small[1],
        small[2],
        small[3],
        small[4],
        small[5],
        big_sums[2],
        small[6],
        big_sums[3],
        small[7],
    )


def solution(mesh):
    return jax.shard_map(
        body,
        mesh=mesh,
        in_specs=(
            P("shard", "ctx", None),
            P("shard", "ctx"),
            P(),
            P(),
            P(None, "shard", "tp"),
            P(None, "tp"),
            P("tp", "shard"),
            P(),
            P(),
            P(),
            P("shard", "tp"),
            P("tp"),
            P("tp", "shard"),
            P(),
            P("shard", "ctx", None),
        ),
        out_specs=(
            P("shard", "ctx", None),
            P("shard", "ctx", None),
            P(None, "shard", "tp"),
            P(None, "tp"),
            P("tp", "shard"),
            P(),
            P(),
            P(),
            P(),
            P(),
            P("shard", "tp"),
            P("tp"),
            P("tp", "shard"),
            P(),
        ),
        check_vma=False,
    )
```

profile of v0, /device:TPU:0, one launch (start us, length us, event | category | flops | bytes accessed | tf_op | source)
XLA Modules:
  0.0 626.5 jit_solution(8793724352426675898)
XLA Ops:
  8.0 0.8 slice_reduce_fusion
  8.8 1.4 convert_reduce_fusion.2
  10.9 6.2 all-gather
  17.2 14.5 %all_gather.25 = bf16[256,1024]{1,0:T(8,128)(2,1)S(1)} all-gather(bf16[256,512]{1,0:T(8,128)(2,1)S(1)} %copy-done.19), channel_id=1, replica_groups=mesh['shard'=2,'ctx'=4,'tp'=4] {'shard'}, dimensions={1}, use_global_device_ids=true | all-gather | bytes 786432 | tf_op jit(solution)/shard_map/all_gather | solution.py:55
  31.7 1.7 bitcast_subtract_fusion
  33.4 10.4 %all-gather.5.cloned.1.call-done = bf16[3,1024,256]{2,1,0:T(8,128)(2,1)} async-done(((bf16[3,512,256]{2,1,0:T(8,128)(2,1)}), bf16[3,1024,256]{2,1,0:T(8,128)(2,1)}) %all-gather.5.cloned.1.call-update) | async-done | bytes 1572880 | tf_op jit(solution)/shard_map/all_gather | solution.py:54
  43.7 2.3 convolution_bitcast_fusion
  46.8 0.8 fusion.55
  47.6 1.4 squeeze.8
  49.0 0.9 add_convert_fusion.2
  50.0 1.3 copy.66
  51.3 11.4 %all_gather.24 = bf16[3,608,256]{2,1,0:T(8,128)(2,1)} all-gather(bf16[3,152,256]{2,1,0:T(8,128)(2,1)} %bitcast.92), channel_id=1, replica_groups=mesh['shard'=2,'ctx'=4,'tp'=4] {'ctx'}, dimensions={1}, use_global_device_ids=true | all-gather | bytes 1167360 | tf_op jit(solution)/shard_map/all_gather | solution.py:72
  62.7 1.5 copy.65
  64.3 10.0 %all_gather.22 = bf16[3,608,256]{2,1,0:T(8,128)(2,1)} all-gather(bf16[3,152,256]{2,1,0:T(8,128)(2,1)S(1)} %add_convert_fusion.3), channel_id=1, replica_groups=mesh['shard'=2,'ctx'=4,'tp'=4] {'ctx'}, dimensions={1}, use_global_device_ids=true | all-gather | bytes 1167360 | tf_op jit(solution)/shard_map/all_gather | solution.py:73
  74.2 2.2 copy.63
  76.5 1.1 fusion
  77.6 1.5 exponential_reduce_fusion
  79.7 1.3 fusion.36
  81.6 1.3 convolution_convert_fusion.7
  84.5 47.4 %all-reduce.12.cloned.1.call-done = bf16[456,1024]{1,0:T(8,128)(2,1)} async-done(((bf16[456,1024]{1,0:T(8,128)(2,1)}), bf16[456,1024]{1,0:T(8,128)(2,1)}) %all-reduce.12.cloned.1.call-update) | async-done | bytes 933904 | tf_op jit(solution)/shard_map/psum | solution.py:100
  131.9 1.5 bitcast_add_fusion
  135.1 30.7 %all-gather.7.cloned.1.call-done = bf16[1024,1024]{1,0:T(8,128)(2,1)} async-done(((bf16[512,1024]{1,0:T(8,128)(2,1)}), bf16[1024,1024]{1,0:T(8,128)(2,1)}) %all-gather.7.cloned.1.call-update) | async-done | bytes 2097168 | tf_op jit(solution)/shard_map/all_gather | solution.py:58
  165.8 7.8 %fusion.18 = (bf16[456,1024]{1,0:T(8,128)(2,1)}, f32[456,1024]{1,0:T(8,128)}) fusion(f32[1024]{0:T(1024)S(1)} %copy-done.28, bf16[1024,1024]{1,0:T(8,128)(2,1)} %all-gather.7.cloned.1.call-done, f32[456,1024]{1,0:T(8,128)S(1)} %subtract_multiply_fusion, f32[1024]{0:T(1024)S(1)} %copy-done.29, f32[1024]{0:T(1024)S(1)} %copy-done.22), kind=kOutput, calls=%fused_computation.33 | convolution fusion | flops 988520448 | bytes 6778880 | tf_op jit(solution)/shard_map/dot_general | solution.py:104
  173.6 26.7 %all-gather.9.cloned.1.call-done = bf16[1024,1024]{1,0:T(8,128)(2,1)} async-done(((bf16[1024,512]{1,0:T(8,128)(2,1)}), bf16[1024,1024]{1,0:T(8,128)(2,1)}) %all-gather.9.cloned.1.call-update) | async-done | bytes 2097168 | tf_op jit(solution)/shard_map/all_gather | solution.py:59
  200.3 4.3 fusion.57
  204.6 0.9 copy-done.31
  205.5 2.1 convolution_convert_fusion.5
  207.7 48.7 %all-reduce.14.cloned.1.call-done = bf16[456,1024]{1,0:T(8,128)(2,1)} async-done(((bf16[456,1024]{1,0:T(8,128)(2,1)}), bf16[456,1024]{1,0:T(8,128)(2,1)}) %all-reduce.14.cloned.1.call-update) | async-done | bytes 933904 | tf_op jit(solution)/shard_map/psum | solution.py:118
  256.4 2.0 fusion.24
  258.5 2.1 fusion.53
  260.6 1.1 convolution_convert_fusion.10
  261.7 1.2 reshape.161
  262.9 1.1 copy.68
  264.0 4.8 convolution_convert_fusion.3
  268.8 5.0 multiply_reduce_fusion
  273.8 3.3 copy.74
  277.1 4.5 multiply_convert_fusion
  281.7 1.7 convolution_convert_fusion.4
  283.4 3.4 copy.71
  287.1 1.3 convolution_convert_fusion.8
  288.4 4.4 convolution_convert_fusion.1
  292.9 4.1 convolution_convert_fusion
  298.8 3.8 fusion.56
  302.6 1.3 copy.69
  304.3 39.7 %all-reduce.20.cloned.1.call-done = (bf16[3,608,256]{2,0,1:T(4,128)(2,1)}, bf16[3,608,256]{2,0,1:T(4,128)(2,1)}) async-done(((bf16[3,608,256]{2,0,1:T(4,128)(2,1)}, bf16[3,608,256]{2,0,1:T(4,128)(2,1)}), (bf16[3,608,256]{2,0,1:T(4,128)(2,1)}, bf16[3,608,256]{2,0,1:T(4,128)(2,1)})) %all-reduce.20.cloned.1.call-update) | async-done | bytes 1867792
  343.9 1.2 constant_dynamic-slice_fusion.1
  345.1 1.3 convert_reduce_fusion.4
  346.4 2.2 fusion.35
  348.7 4.1 convolution_convert_fusion.6
  352.8 1.9 bitcast_convert_fusion
  354.7 6.7 %reduce-scatter.7.cloned.1.call-done = bf16[256,512]{1,0:T(8,128)(2,1)} async-done(((bf16[256,1024]{1,0:T(8,128)(2,1)}), bf16[256,512]{1,0:T(8,128)(2,1)}) %reduce-scatter.7.cloned.1.call-update) | async-done | bytes 262160 | tf_op jit(solution)/shard_map/reduce_scatter | solution.py:179
  361.5 34.8 %reduce-scatter.9.cloned.1.call-done = bf16[512,1024]{1,0:T(8,128)(2,1)} async-done(((bf16[1024,1024]{1,0:T(8,128)(2,1)}), bf16[512,1024]{1,0:T(8,128)(2,1)}) %reduce-scatter.9.cloned.1.call-update) | async-done | bytes 1048592 | tf_op jit(solution)/shard_map/reduce_scatter | solution.py:182
  396.2 34.8 %reduce-scatter.11.cloned.1.call-done = bf16[1024,512]{1,0:T(8,128)(2,1)} async-done(((bf16[1024,1024]{1,0:T(8,128)(2,1)}), bf16[1024,512]{1,0:T(8,128)(2,1)}) %reduce-scatter.11.cloned.1.call-update) | async-done | bytes 1048592 | tf_op jit(solution)/shard_map/reduce_scatter | solution.py:185
  431.0 28.8 %reduce-scatter.5.cloned.1.call-done = bf16[3,512,256]{1,2,0:T(8,128)(2,1)} async-done(((bf16[3,1024,256]{1,2,0:T(8,128)(2,1)}), bf16[3,512,256]{1,2,0:T(8,128)(2,1)}) %reduce-scatter.5.cloned.1.call-update) | async-done | bytes 786448 | tf_op jit(solution)/shard_map/reduce_scatter | solution.py:176
  459.8 1.4 convert_reduce_fusion.3
  461.3 80.3 %all-reduce.16.cloned.1.call-done = (bf16[456,1024]{1,0:T(8,128)(2,1)}, bf16[456,1024]{1,0:T(8,128)(2,1)}) async-done(((bf16[456,1024]{1,0:T(8,128)(2,1)}, bf16[456,1024]{1,0:T(8,128)(2,1)}), (bf16[456,1024]{1,0:T(8,128)(2,1)}, bf16[456,1024]{1,0:T(8,128)(2,1)})) %all-reduce.16.cloned.1.call-update) | async-done | bytes 1867792 | tf_op jit(solution)/shard_map/psum | solution.py:107
  541.6 2.8 fusion.6
  544.4 24.2 %all-reduce.2 = (f32[2,256]{1,0:T(2,128)}, f32[1024]{0:T(1024)}, f32[1024]{0:T(1024)}, f32[1024]{0:T(1024)}, f32[1024]{0:T(1024)}, /*index=5*/f32[1024]{0:T(1024)}, f32[1024]{0:T(1024)}, f32[1024]{0:T(1024)}) all-reduce(f32[2,256]{1,0:T(2,128)S(1)} %pad_maximum_fusion.3, ...), channel_id=1, replica_groups=mesh['shard'=2,'ctx'=4,'tp'=4] {'shard','ctx'}, use_global_device_ids=true, to_apply=%region_21.22 | all-reduce | flops 7680 | bytes 61440 | tf_op jit(solution)/shard_map/psum | solution.py:156
  568.6 4.5 fusion.10
  573.1 38.9 %all-reduce.18.cloned.1.call-done = (bf16[3,512,256]{1,2,0:T(8,128)(2,1)}, bf16[256,512]{1,0:T(8,128)(2,1)}, bf16[512,1024]{1,0:T(8,128)(2,1)}, bf16[1024,512]{1,0:T(8,128)(2,1)}) async-done(((bf16[3,512,256]{1,2,0:T(8,128)(2,1)}, bf16[256,512]{1,0:T(8,128)(2,1)}, bf16[512,1024]{1,0:T(8,128)(2,1)}, bf16[1024,512]{1,0:T(8,128)(2,1)}), (bf16[3,512,256]{1,2,0:T(8,128)(2,1)}, bf16[256,512]{1,0:T(8,128)(2,1)}, ...) | async-done | bytes 3145744 | tf_op jit(solution)/shard_map/psum | solution.py:170
  612.0 1.9 convert_element_type.182
  613.9 2.5 copy.76
  616.5 1.6 convert_element_type.184
  618.0 1.6 convert_element_type.186
  (115 shorter events, 9.0 us)
Async XLA Ops:
  7.2 3.2 copy-start.1
  7.2 3.7 copy-start.24
  7.2 10.0 %copy-start.19 = (bf16[256,512]{1,0:T(8,128)(2,1)S(1)}, bf16[256,512]{1,0:T(8,128)(2,1)}, u32[]{:S(2)}) copy-start(bf16[256,512]{1,0:T(8,128)(2,1)} %param.21) | copy-start | bytes 786436
  7.2 24.5 %copy-start.21 = (f32[1024]{0:T(1024)S(1)}, f32[1024]{0:T(1024)}, u32[]{:S(2)}) copy-start(f32[1024]{0:T(1024)} %param.17) | copy-start | bytes 12292
  7.2 24.5 %copy-start.25 = (f32[1024]{0:T(1024)S(1)}, f32[1024]{0:T(1024)}, u32[]{:S(2)}) copy-start(f32[1024]{0:T(1024)} %param.18) | copy-start | bytes 12292
  7.2 36.5 %all-gather.5.cloned.1.call-start = ((), (), s32[]{:S(2)}) async-start(), calls=%async_computation.4 | async-start | bytes 2359296 | tf_op jit(solution)/shard_map/all_gather | solution.py:54
  8.0 124.0 %all-reduce.12.cloned.1.call-start = ((), (), s32[]{:S(2)}) async-start(), calls=%async_computation.5 | async-start | bytes 1867776 | tf_op jit(solution)/shard_map/psum | solution.py:100
  33.3 12.7 %copy-start.17 = (bf16[456,1024]{1,0:T(8,128)(2,1)}, bf16[456,1024]{1,0:T(8,128)(2,1)S(1)}, u32[]{:S(2)}) copy-start(bf16[456,1024]{1,0:T(8,128)(2,1)S(1)} %get-tuple-element.101) | copy-start | bytes 2801668
  51.2 25.2 %copy-start.6 = (bf16[3,152,4,64]{1,3,2,0:T(8,128)(2,1)}, bf16[3,152,4,64]{1,3,2,0:T(8,128)(2,1)S(1)}, u32[]{:S(2)}) copy-start(bf16[3,152,4,64]{1,3,2,0:T(8,128)(2,1)S(1)} %copy.66) | copy-start | bytes 700420
  64.2 12.2 %copy-start.4 = (bf16[3,608,256]{1,2,0:T(8,128)(2,1)}, bf16[3,608,256]{1,2,0:T(8,128)(2,1)S(1)}, u32[]{:S(2)}) copy-start(bf16[3,608,256]{1,2,0:T(8,128)(2,1)S(1)} %copy.65) | copy-start | bytes 2801668
  77.6 2.1 copy-start
  77.6 2.1 copy-start.8
  81.6 2.7 copy-start.12
  83.0 82.8 %all-gather.7.cloned.1.call-start = ((), (), s32[]{:S(2)}) async-start(), calls=%async_computation.6 | async-start | bytes 3145728 | tf_op jit(solution)/shard_map/all_gather | solution.py:58
  83.7 116.6 %all-gather.9.cloned.1.call-start = ((), (), s32[]{:S(2)}) async-start(), calls=%async_computation.7 | async-start | bytes 3145728 | tf_op jit(solution)/shard_map/all_gather | solution.py:59
  84.3 49.2 %copy-start.20 = (f32[1024]{0:T(1024)S(1)}, f32[1024]{0:T(1024)}, u32[]{:S(2)}) copy-start(f32[1024]{0:T(1024)} %param.22) | copy-start | bytes 12292
  84.3 172.1 %all-reduce.14.cloned.1.call-start = ((), (), s32[]{:S(2)}) async-start(), calls=%async_computation.8 | async-start | bytes 1867776 | tf_op jit(solution)/shard_map/psum | solution.py:118
  133.5 1.2 copy-start.5
  134.7 31.1 %copy-start.22 = (f32[1024]{0:T(1024)S(1)}, f32[1024]{0:T(1024)}, u32[]{:S(2)}) copy-start(f32[1024]{0:T(1024)} %param.23) | copy-start | bytes 12292
  134.7 31.1 %copy-start.28 = (f32[1024]{0:T(1024)S(1)}, f32[1024]{0:T(1024)}, u32[]{:S(2)}) copy-start(f32[1024]{0:T(1024)} %param.26) | copy-start | bytes 12292
  134.7 31.1 %copy-start.29 = (f32[1024]{0:T(1024)S(1)}, f32[1024]{0:T(1024)}, u32[]{:S(2)}) copy-start(f32[1024]{0:T(1024)} %param.24) | copy-start | bytes 12292
  135.1 121.4 %copy-start.3 = (f32[456,1024]{1,0:T(8,128)}, f32[456,1024]{1,0:T(8,128)S(1)}, u32[]{:S(2)}) copy-start(f32[456,1024]{1,0:T(8,128)S(1)} %subtract_multiply_fusion) | copy-start | bytes 5603332
  200.3 5.2 copy-start.26
  204.6 0.9 copy-start.31
  207.6 136.3 %all-reduce.20.cloned.1.call-start = ((), (), s32[]{:S(2)}) async-start(), calls=%async_computation.15 | async-start | bytes 4980736
  256.4 2.0 copy-start.10
  256.4 2.0 copy-start.11
  264.0 4.8 copy-start.9
  264.0 4.8 copy-start.14
  277.1 4.5 copy-start.7
  281.7 1.7 copy-start.2
  283.4 3.7 copy-start.13
  286.8 74.7 %reduce-scatter.7.cloned.1.call-start = ((), (), s32[]{:S(2)}) async-start(), calls=%async_computation.10 | async-start | bytes 786432 | tf_op jit(solution)/shard_map/reduce_scatter | solution.py:179
  288.4 107.9 %reduce-scatter.9.cloned.1.call-start = ((), (), s32[]{:S(2)}) async-start(), calls=%async_computation.11 | async-start | bytes 3145728 | tf_op jit(solution)/shard_map/reduce_scatter | solution.py:182
  292.8 138.2 %reduce-scatter.11.cloned.1.call-start = ((), (), s32[]{:S(2)}) async-start(), calls=%async_computation.12 | async-start | bytes 3145728 | tf_op jit(solution)/shard_map/reduce_scatter | solution.py:185
  297.0 0.7 copy-start.30
  297.0 162.8 %reduce-scatter.5.cloned.1.call-start = ((), (), s32[]{:S(2)}) async-start(), calls=%async_computation.9 | async-start | bytes 2359296 | tf_op jit(solution)/shard_map/reduce_scatter | solution.py:176
  343.9 2.5 copy-start.18
  348.7 192.9 %all-reduce.16.cloned.1.call-start = ((), (), s32[]{:S(2)}) async-start(), calls=%async_computation.13 | async-start | bytes 3735552 | tf_op jit(solution)/shard_map/psum | solution.py:107
  348.7 4.1 copy-start.27
  354.7 257.3 %all-reduce.18.cloned.1.call-start = ((), (), s32[]{:S(2)}) async-start(), calls=%async_computation.14 | async-start | bytes 6291456 | tf_op jit(solution)/shard_map/psum | solution.py:170
  541.6 27.0 %copy-start.23 = (f32[1024]{0:T(1024)S(1)}, f32[1024]{0:T(1024)}, u32[]{:S(2)}) copy-start(f32[1024]{0:T(1024)} %param.28) | copy-start | bytes 12292
  612.0 4.4 copy-start.16
  616.5 1.6 copy-start.15
Sparse Core Ops, SparseCore 0:
  9.6 34.1 all-gather.4
  83.1 48.8 all-reduce.11
  133.5 32.2 all-gather.6
  167.2 33.0 all-gather.8
  207.8 48.6 all-reduce.13
  286.9 56.9 all-reduce.19
  346.7 14.6 reduce-scatter.6
  364.3 31.8 reduce-scatter.8
  399.0 31.8 reduce-scatter.10
  433.6 26.1 reduce-scatter.4
  462.8 78.6 all-reduce.15
  544.0 67.9 all-reduce.17
where the time goes:
time: 628 us; the launch traced here: 627 us
  waiting for transfers between devices  430 us (68%)
  blocking collectives  66.3 us (11%)
  matrix products  54.6 us (9%)
  other arithmetic  32.1 us (5%)
  local copies, waits for them, and re-layouts  27.5 us (4%)
  between operations  15.3 us (2%)
    psum x1, waiting for transfers between devices, body(): lax.psum(mlp_part.astype(jnp.bfloat16), 'tp').astype(jnp.float32)  80.3 us
    psum x1, waiting for transfers between devices, body(): lax.psum(norm2_part.astype(jnp.bfloat16), 'tp').astype(jnp.float32)  48.7 us
    psum x1, waiting for transfers between devices, body(): lax.psum(attn_part.astype(jnp.bfloat16), 'tp').astype(jnp.float32)  47.4 us
    unnamed x13, waiting for transfers between devices  41.7 us
    psum x1, waiting for transfers between devices, body(): lax.psum(grad_qkv.astype(jnp.bfloat16), 'ctx').astype(jnp.float32)  38.9 us
    reduce_scatter x1, waiting for transfers between devices, body(): lax.psum_scatter(summed[3].astype(jnp.bfloat16), 'shard', scatter_dimensi...  34.8 us
    reduce_scatter x1, waiting for transfers between devices, body(): lax.psum_scatter(summed[2].astype(jnp.bfloat16), 'shard', scatter_dimensi...  34.8 us
    all_gather x1, waiting for transfers between devices, body(): lax.all_gather(w_up, 'shard', axis=0, tiled=True)  30.7 us
  transfers between devices with their start and end apart: 12, of which 12 were waited for; matrix products, arithmetic and copies ran while one was open for 8% of the time, Pallas kernels for 0%

commit v1 on v0

--- a/solution.py
+++ b/solution.py
@@ -6,6 +6,30 @@
 
 HD = 64
 NEG_FILL = -1e30
+
+
+def spans_connect(a0, across, which_dim):
+    main, upper, block_last = (
+        lax.psum(1, axis_name=across),
+        lax.axis_index(across),
+        a0.shape[which_dim],
+    )
+    carry_in, formed = (a0, 1)
+    while formed < main:
+        carry_in = jnp.concatenate(
+            [
+                carry_in,
+                lax.ppermute(
+                    carry_in,
+                    axis_name=across,
+                    perm=[(idx, (idx - formed) % main) for idx in range(main)],
+                ),
+            ],
+            which_dim,
+        )
+        formed = 2 * formed
+    z_new = jnp.roll(carry_in, upper * block_last, which_dim)
+    return z_new
 
 
 def normalize(values, gain, shift):
@@ -56,7 +80,7 @@
     )
     up_full, down_full = (
         lax.all_gather(w_up, "shard", axis=0, tiled=True),
-        lax.all_gather(w_down, "shard", axis=1, tiled=True),
+        spans_connect(w_down, "shard", 1),
     )
     local_width = out_full.shape[0]
     local_heads = local_width // HD

time: 628 us -> 598 us (0.952)
  waiting for transfers between devices: 430 us -> 397 us
    psum x1, waiting for transfers between devices: 47.4 us -> 19.2 us  [body(): lax.psum(attn_part.astype(jnp.bfloat16), 'tp').astype(jnp.float32)]
    all_gather x1 -> x0, waiting for transfers between devices: 26.7 us -> none  [body(): lax.all_gather(w_down, 'shard', axis=1, tiled=True)]
    ppermute x0 -> x1, waiting for transfers between devices: none -> 23.8 us  [spans_connect(): lax.ppermute(carry_in, axis_name=across, perm=[(idx, (idx - formed) % mai...]
    unnamed x13 -> x12, waiting for transfers between devices: 41.7 us -> 40.6 us
where the time goes in v1:
time: 598 us; the launch traced here: 597 us
  waiting for transfers between devices  397 us (66%)
  blocking collectives  66.3 us (11%)
  matrix products  52.1 us (9%)
  other arithmetic  36.2 us (6%)
  local copies, waits for them, and re-layouts  27.7 us (5%)
  between operations  15 us (3%)
    psum x1, waiting for transfers between devices, body(): lax.psum(mlp_part.astype(jnp.bfloat16), 'tp').astype(jnp.float32)  80.7 us
    psum x1, waiting for transfers between devices, body(): lax.psum(norm2_part.astype(jnp.bfloat16), 'tp').astype(jnp.float32)  48.5 us
    unnamed x12, waiting for transfers between devices  40.6 us
    psum x1, waiting for transfers between devices, body(): lax.psum(grad_qkv.astype(jnp.bfloat16), 'ctx').astype(jnp.float32)  39.1 us
    reduce_scatter x1, waiting for transfers between devices, body(): lax.psum_scatter(summed[2].astype(jnp.bfloat16), 'shard', scatter_dimensi...  34.8 us
    reduce_scatter x1, waiting for transfers between devices, body(): lax.psum_scatter(summed[3].astype(jnp.bfloat16), 'shard', scatter_dimensi...  34.2 us
    all_gather x1, waiting for transfers between devices, body(): lax.all_gather(w_up, 'shard', axis=0, tiled=True)  30.7 us
    reduce_scatter x1, waiting for transfers between devices, body(): lax.psum_scatter(summed[0].astype(jnp.bfloat16), 'shard', scatter_dimensi...  29 us
  transfers between devices with their start and end apart: 12, of which 12 were waited for; matrix products, arithmetic and copies ran while one was open for 8% of the time, Pallas kernels for 0%

profile of v1, /device:TPU:0, one launch (start us, length us, event | category | flops | bytes accessed | tf_op | source)
XLA Modules:
  0.0 597.1 jit_solution(2427344567071403338)
XLA Ops:
  8.8 1.4 convert_reduce_fusion.2
  10.9 6.2 %all-gather = bf16[4,152,3]{1,2,0:T(4,128)(2,1)S(1)} all-gather(bf16[1,152,3]{1,2,0:T(4,128)(2,1)S(1)} %fusion.49), channel_id=1, replica_groups=mesh['shard'=2,'ctx'=4,'tp'=4] {'ctx'}, dimensions={0}, use_global_device_ids=true | all-gather | bytes 4560 | tf_op jit(solution)/shard_map/all_gather | solution.py:98
  17.2 14.5 %all_gather.22 = bf16[256,1024]{1,0:T(8,128)(2,1)S(1)} all-gather(bf16[256,512]{1,0:T(8,128)(2,1)S(1)} %copy-done.22), channel_id=1, replica_groups=mesh['shard'=2,'ctx'=4,'tp'=4] {'shard'}, dimensions={1}, use_global_device_ids=true | all-gather | bytes 786432 | tf_op jit(solution)/shard_map/all_gather | solution.py:79
  31.7 1.7 bitcast_subtract_fusion
  33.3 10.4 %all-gather.4.cloned.1.call-done = bf16[3,1024,256]{2,1,0:T(8,128)(2,1)} async-done(((bf16[3,512,256]{2,1,0:T(8,128)(2,1)}), bf16[3,1024,256]{2,1,0:T(8,128)(2,1)}) %all-gather.4.cloned.1.call-update) | async-done | bytes 1572880 | tf_op jit(solution)/shard_map/all_gather | solution.py:78
  43.7 2.3 convolution_bitcast_fusion
  47.6 1.4 squeeze.8
  49.0 0.9 add_convert_fusion.2
  50.0 1.3 copy.66
  51.3 11.4 %all_gather.21 = bf16[3,608,256]{2,1,0:T(8,128)(2,1)} all-gather(bf16[3,152,256]{2,1,0:T(8,128)(2,1)} %bitcast.94), channel_id=1, replica_groups=mesh['shard'=2,'ctx'=4,'tp'=4] {'ctx'}, dimensions={1}, use_global_device_ids=true | all-gather | bytes 1167360 | tf_op jit(solution)/shard_map/all_gather | solution.py:96
  62.7 1.5 copy.65
  64.3 10.0 %all_gather.19 = bf16[3,608,256]{2,1,0:T(8,128)(2,1)} all-gather(bf16[3,152,256]{2,1,0:T(8,128)(2,1)S(1)} %add_convert_fusion.3), channel_id=1, replica_groups=mesh['shard'=2,'ctx'=4,'tp'=4] {'ctx'}, dimensions={1}, use_global_device_ids=true | all-gather | bytes 1167360 | tf_op jit(solution)/shard_map/all_gather | solution.py:97
  74.3 2.2 copy.63
  76.5 1.1 fusion
  77.6 1.5 exponential_reduce_fusion
  79.8 1.3 fusion.39
  81.8 1.3 convolution_convert_fusion.7
  83.2 1.5 collective-permute-start
  85.0 23.8 %collective-permute-done = bf16[1024,512]{1,0:T(8,128)(2,1)} collective-permute-done((bf16[1024,512]{1,0:T(8,128)(2,1)S(1)}, bf16[1024,512]{1,0:T(8,128)(2,1)}, u32[]{:S(2)}, u32[]{:S(2)}) %collective-permute-start) | collective-permute-done | bytes 1048608 | tf_op jit(solution)/shard_map/ppermute | solution.py:22
  108.8 4.1 fusion.10
  112.9 19.2 %all-reduce.12.cloned.1.call-done = bf16[456,1024]{1,0:T(8,128)(2,1)} async-done(((bf16[456,1024]{1,0:T(8,128)(2,1)}), bf16[456,1024]{1,0:T(8,128)(2,1)}) %all-reduce.12.cloned.1.call-update) | async-done | bytes 933904 | tf_op jit(solution)/shard_map/psum | solution.py:124
  132.1 1.5 bitcast_add_fusion
  135.2 30.7 %all-gather.6.cloned.1.call-done = bf16[1024,1024]{1,0:T(8,128)(2,1)} async-done(((bf16[512,1024]{1,0:T(8,128)(2,1)}), bf16[1024,1024]{1,0:T(8,128)(2,1)}) %all-gather.6.cloned.1.call-update) | async-done | bytes 2097168 | tf_op jit(solution)/shard_map/all_gather | solution.py:82
  165.9 7.7 %fusion.21 = (bf16[456,1024]{1,0:T(8,128)(2,1)}, f32[456,1024]{1,0:T(8,128)S(1)}) fusion(f32[1024]{0:T(1024)S(1)} %copy-done.31, bf16[1024,1024]{1,0:T(8,128)(2,1)} %all-gather.6.cloned.1.call-done, f32[456,1024]{1,0:T(8,128)S(1)} %subtract_multiply_fusion, f32[1024]{0:T(1024)S(1)} %copy-done.32, f32[1024]{0:T(1024)S(1)} %copy-done.25), kind=kOutput, calls=%fused_computation.40 | convolution fusion | flops 988520448 | bytes 6778880 | tf_op jit(solution)/shard_map/dot_general | solution.py:128
  173.6 1.9 fusion.60
  175.5 0.9 copy-done.34
  176.5 2.1 convolution_convert_fusion.5
  178.9 48.5 %all-reduce.14.cloned.1.call-done = bf16[456,1024]{1,0:T(8,128)(2,1)} async-done(((bf16[456,1024]{1,0:T(8,128)(2,1)}), bf16[456,1024]{1,0:T(8,128)(2,1)}) %all-reduce.14.cloned.1.call-update) | async-done | bytes 933904 | tf_op jit(solution)/shard_map/psum | solution.py:142
  227.4 2.0 fusion.27
  229.4 2.1 fusion.56
  231.6 1.1 convolution_convert_fusion.10
  232.7 1.2 reshape.161
  233.9 1.1 copy.68
  235.0 4.8 convolution_convert_fusion.3
  239.8 4.9 multiply_reduce_fusion
  244.8 3.3 copy.74
  248.1 4.5 multiply_convert_fusion
  252.6 1.7 convolution_convert_fusion.4
  254.3 3.4 copy.71
  257.8 1.3 convolution_convert_fusion.8
  259.1 4.4 convolution_convert_fusion.1
  263.6 4.2 convolution_convert_fusion
  269.7 3.8 fusion.59
  273.4 1.3 copy.69
  275.1 39.8 %all-reduce.20.cloned.1.call-done = (bf16[3,608,256]{2,0,1:T(4,128)(2,1)}, bf16[3,608,256]{2,0,1:T(4,128)(2,1)}) async-done(((bf16[3,608,256]{2,0,1:T(4,128)(2,1)}, bf16[3,608,256]{2,0,1:T(4,128)(2,1)}), (bf16[3,608,256]{2,0,1:T(4,128)(2,1)}, bf16[3,608,256]{2,0,1:T(4,128)(2,1)})) %all-reduce.20.cloned.1.call-update) | async-done | bytes 1867792
  314.9 1.2 constant_dynamic-slice_fusion.1
  316.0 1.3 convert_reduce_fusion.4
  317.3 2.2 fusion.38
  319.9 4.1 convolution_convert_fusion.6
  324.0 1.9 bitcast_convert_fusion
  325.9 6.3 %reduce-scatter.7.cloned.1.call-done = bf16[256,512]{1,0:T(8,128)(2,1)} async-done(((bf16[256,1024]{1,0:T(8,128)(2,1)}), bf16[256,512]{1,0:T(8,128)(2,1)}) %reduce-scatter.7.cloned.1.call-update) | async-done | bytes 262160 | tf_op jit(solution)/shard_map/reduce_scatter | solution.py:203
  332.3 34.8 %reduce-scatter.9.cloned.1.call-done = bf16[512,1024]{1,0:T(8,128)(2,1)} async-done(((bf16[1024,1024]{1,0:T(8,128)(2,1)}), bf16[512,1024]{1,0:T(8,128)(2,1)}) %reduce-scatter.9.cloned.1.call-update) | async-done | bytes 1048592 | tf_op jit(solution)/shard_map/reduce_scatter | solution.py:206
  367.0 34.2 %reduce-scatter.11.cloned.1.call-done = bf16[1024,512]{1,0:T(8,128)(2,1)} async-done(((bf16[1024,1024]{1,0:T(8,128)(2,1)}), bf16[1024,512]{1,0:T(8,128)(2,1)}) %reduce-scatter.11.cloned.1.call-update) | async-done | bytes 1048592 | tf_op jit(solution)/shard_map/reduce_scatter | solution.py:209
  401.2 29.0 %reduce-scatter.5.cloned.1.call-done = bf16[3,512,256]{1,2,0:T(8,128)(2,1)} async-done(((bf16[3,1024,256]{1,2,0:T(8,128)(2,1)}), bf16[3,512,256]{1,2,0:T(8,128)(2,1)}) %reduce-scatter.5.cloned.1.call-update) | async-done | bytes 786448 | tf_op jit(solution)/shard_map/reduce_scatter | solution.py:200
  430.2 1.4 convert_reduce_fusion.3
  431.7 80.7 %all-reduce.16.cloned.1.call-done = (bf16[456,1024]{1,0:T(8,128)(2,1)}, bf16[456,1024]{1,0:T(8,128)(2,1)}) async-done(((bf16[456,1024]{1,0:T(8,128)(2,1)}, bf16[456,1024]{1,0:T(8,128)(2,1)}), (bf16[456,1024]{1,0:T(8,128)(2,1)}, bf16[456,1024]{1,0:T(8,128)(2,1)})) %all-reduce.16.cloned.1.call-update) | async-done | bytes 1867792 | tf_op jit(solution)/shard_map/psum | solution.py:131
  512.3 2.8 fusion.6
  515.1 24.2 %all-reduce.2 = (f32[2,256]{1,0:T(2,128)}, f32[1024]{0:T(1024)}, f32[1024]{0:T(1024)}, f32[1024]{0:T(1024)}, f32[1024]{0:T(1024)}, /*index=5*/f32[1024]{0:T(1024)}, f32[1024]{0:T(1024)}, f32[1024]{0:T(1024)}) all-reduce(f32[2,256]{1,0:T(2,128)S(1)} %pad_maximum_fusion.3, ...), channel_id=1, replica_groups=mesh['shard'=2,'ctx'=4,'tp'=4] {'shard','ctx'}, use_global_device_ids=true, to_apply=%region_21.22 | all-reduce | flops 7680 | bytes 61440 | tf_op jit(solution)/shard_map/psum | solution.py:180
  539.4 4.5 fusion.13
  543.9 39.1 %all-reduce.18.cloned.1.call-done = (bf16[3,512,256]{1,2,0:T(8,128)(2,1)}, bf16[256,512]{1,0:T(8,128)(2,1)}, bf16[512,1024]{1,0:T(8,128)(2,1)}, bf16[1024,512]{1,0:T(8,128)(2,1)}) async-done(((bf16[3,512,256]{1,2,0:T(8,128)(2,1)}, bf16[256,512]{1,0:T(8,128)(2,1)}, bf16[512,1024]{1,0:T(8,128)(2,1)}, bf16[1024,512]{1,0:T(8,128)(2,1)}), (bf16[3,512,256]{1,2,0:T(8,128)(2,1)}, bf16[256,512]{1,0:T(8,128)(2,1)}, ...) | async-done | bytes 3145744 | tf_op jit(solution)/shard_map/psum | solution.py:194
  583.0 1.9 convert_element_type.182
  584.9 2.5 copy.76
  587.4 1.6 convert_element_type.184
  589.0 1.6 convert_element_type.186
  (121 shorter events, 9.8 us)
Async XLA Ops:
  7.2 3.2 copy-start.1
  7.2 3.7 copy-start.27
  7.2 10.0 %copy-start.22 = (bf16[256,512]{1,0:T(8,128)(2,1)S(1)}, bf16[256,512]{1,0:T(8,128)(2,1)}, u32[]{:S(2)}) copy-start(bf16[256,512]{1,0:T(8,128)(2,1)} %param.21) | copy-start | bytes 786436
  7.2 24.5 %copy-start.24 = (f32[1024]{0:T(1024)S(1)}, f32[1024]{0:T(1024)}, u32[]{:S(2)}) copy-start(f32[1024]{0:T(1024)} %param.17) | copy-start | bytes 12292
  7.2 24.5 %copy-start.28 = (f32[1024]{0:T(1024)S(1)}, f32[1024]{0:T(1024)}, u32[]{:S(2)}) copy-start(f32[1024]{0:T(1024)} %param.18) | copy-start | bytes 12292
  7.2 36.5 %all-gather.4.cloned.1.call-start = ((), (), s32[]{:S(2)}) async-start(), calls=%async_computation.4 | async-start | bytes 2359296 | tf_op jit(solution)/shard_map/all_gather | solution.py:78
  8.0 124.1 %all-reduce.12.cloned.1.call-start = ((), (), s32[]{:S(2)}) async-start(), calls=%async_computation.5 | async-start | bytes 1867776 | tf_op jit(solution)/shard_map/psum | solution.py:124
  33.3 12.7 %copy-start.20 = (bf16[456,1024]{1,0:T(8,128)(2,1)}, bf16[456,1024]{1,0:T(8,128)(2,1)S(1)}, u32[]{:S(2)}) copy-start(bf16[456,1024]{1,0:T(8,128)(2,1)S(1)} %get-tuple-element.101) | copy-start | bytes 2801668
  51.2 25.2 %copy-start.6 = (bf16[3,152,4,64]{1,3,2,0:T(8,128)(2,1)}, bf16[3,152,4,64]{1,3,2,0:T(8,128)(2,1)S(1)}, u32[]{:S(2)}) copy-start(bf16[3,152,4,64]{1,3,2,0:T(8,128)(2,1)S(1)} %copy.66) | copy-start | bytes 700420
  64.2 12.2 %copy-start.4 = (bf16[3,608,256]{1,2,0:T(8,128)(2,1)}, bf16[3,608,256]{1,2,0:T(8,128)(2,1)S(1)}, u32[]{:S(2)}) copy-start(bf16[3,608,256]{1,2,0:T(8,128)(2,1)S(1)} %copy.65) | copy-start | bytes 2801668
  77.6 2.2 copy-start
  77.6 2.2 copy-start.8
  81.4 1.8 copy-start.17
  81.8 31.1 %copy-start.13 = (bf16[456,256]{1,0:T(8,128)(2,1)}, bf16[456,256]{1,0:T(8,128)(2,1)S(1)}, u32[]{:S(2)}) copy-start(bf16[456,256]{1,0:T(8,128)(2,1)S(1)} %reshape.158) | copy-start | bytes 700420
  83.1 82.8 %all-gather.6.cloned.1.call-start = ((), (), s32[]{:S(2)}) async-start(), calls=%async_computation.6 | async-start | bytes 3145728 | tf_op jit(solution)/shard_map/all_gather | solution.py:82
  83.2 25.6 %collective-permute-start = (bf16[1024,512]{1,0:T(8,128)(2,1)S(1)}, bf16[1024,512]{1,0:T(8,128)(2,1)}, u32[]{:S(2)}, u32[]{:S(2)}) collective-permute-start(bf16[1024,512]{1,0:T(8,128)(2,1)S(1)} %copy-done.17), channel_id=1, source_target_pairs={{0,16},{16,0},{1,17},{17,1},{2,18},{18,2},{3,19},{19,3},{4,20},{20... | collective-permute-start | bytes 3145736 | tf_op jit(solution)/shard_map/ppermute | solution.py:22
  84.7 142.7 %all-reduce.14.cloned.1.call-start = ((), (), s32[]{:S(2)}) async-start(), calls=%async_computation.7 | async-start | bytes 1867776 | tf_op jit(solution)/shard_map/psum | solution.py:142
  112.9 20.7 %copy-start.23 = (f32[1024]{0:T(1024)S(1)}, f32[1024]{0:T(1024)}, u32[]{:S(2)}) copy-start(f32[1024]{0:T(1024)} %param.22) | copy-start | bytes 12292
  133.6 1.2 copy-start.5
  134.8 31.1 %copy-start.25 = (f32[1024]{0:T(1024)S(1)}, f32[1024]{0:T(1024)}, u32[]{:S(2)}) copy-start(f32[1024]{0:T(1024)} %param.23) | copy-start | bytes 12292
  134.8 31.1 %copy-start.31 = (f32[1024]{0:T(1024)S(1)}, f32[1024]{0:T(1024)}, u32[]{:S(2)}) copy-start(f32[1024]{0:T(1024)} %param.26) | copy-start | bytes 12292
  134.8 31.1 %copy-start.32 = (f32[1024]{0:T(1024)S(1)}, f32[1024]{0:T(1024)}, u32[]{:S(2)}) copy-start(f32[1024]{0:T(1024)} %param.24) | copy-start | bytes 12292
  135.2 92.2 %copy-start.3 = (f32[456,1024]{1,0:T(8,128)}, f32[456,1024]{1,0:T(8,128)S(1)}, u32[]{:S(2)}) copy-start(f32[456,1024]{1,0:T(8,128)S(1)} %subtract_multiply_fusion) | copy-start | bytes 5603332
  165.9 7.7 %copy-start.10 = (bf16[3,152,1024]{2,1,0:T(8,128)(2,1)S(1)}, bf16[3,152,1024]{2,1,0:T(8,128)(2,1)}, u32[]{:S(2)}) copy-start(bf16[3,152,1024]{2,1,0:T(8,128)(2,1)} %param.29) | copy-start | bytes 2801668
  165.9 7.7 %copy-start.15 = (bf16[1024,1024]{1,0:T(8,128)(2,1)S(1)}, bf16[1024,1024]{1,0:T(8,128)(2,1)}, u32[]{:S(2)}) copy-start(bf16[1024,1024]{1,0:T(8,128)(2,1)} %fusion.10) | copy-start | bytes 6291460
  173.6 2.9 copy-start.29
  175.5 1.0 copy-start.34
  178.6 136.2 %all-reduce.20.cloned.1.call-start = ((), (), s32[]{:S(2)}) async-start(), calls=%async_computation.14 | async-start | bytes 4980736
  227.4 2.0 copy-start.11
  227.4 2.0 copy-start.12
  235.0 4.8 copy-start.9
  235.0 4.8 copy-start.16
  248.1 4.5 copy-start.7
  252.6 1.7 copy-start.2
  254.3 3.4 copy-start.14
  257.7 74.5 %reduce-scatter.7.cloned.1.call-start = ((), (), s32[]{:S(2)}) async-start(), calls=%async_computation.9 | async-start | bytes 786432 | tf_op jit(solution)/shard_map/reduce_scatter | solution.py:203
  259.1 107.9 %reduce-scatter.9.cloned.1.call-start = ((), (), s32[]{:S(2)}) async-start(), calls=%async_computation.10 | async-start | bytes 3145728 | tf_op jit(solution)/shard_map/reduce_scatter | solution.py:206
  263.5 137.6 %reduce-scatter.11.cloned.1.call-start = ((), (), s32[]{:S(2)}) async-start(), calls=%async_computation.11 | async-start | bytes 3145728 | tf_op jit(solution)/shard_map/reduce_scatter | solution.py:209
  267.8 0.7 copy-start.33
  267.8 162.4 %reduce-scatter.5.cloned.1.call-start = ((), (), s32[]{:S(2)}) async-start(), calls=%async_computation.8 | async-start | bytes 2359296 | tf_op jit(solution)/shard_map/reduce_scatter | solution.py:200
  314.8 2.5 copy-start.21
  319.6 192.7 %all-reduce.16.cloned.1.call-start = ((), (), s32[]{:S(2)}) async-start(), calls=%async_computation.12 | async-start | bytes 3735552 | tf_op jit(solution)/shard_map/psum | solution.py:131
  319.9 4.1 copy-start.30
  325.9 257.1 %all-reduce.18.cloned.1.call-start = ((), (), s32[]{:S(2)}) async-start(), calls=%async_computation.13 | async-start | bytes 6291456 | tf_op jit(solution)/shard_map/psum | solution.py:194
  512.3 27.0 %copy-start.26 = (f32[1024]{0:T(1024)S(1)}, f32[1024]{0:T(1024)}, u32[]{:S(2)}) copy-start(f32[1024]{0:T(1024)} %param.28) | copy-start | bytes 12292
  583.0 4.4 copy-start.19
  587.4 1.6 copy-start.18
Sparse Core Ops, SparseCore 0:
  9.6 34.1 all-gather.3
  83.3 48.7 all-reduce.11
  133.6 32.2 all-gather.5
  178.7 48.6 all-reduce.13
  257.9 56.9 all-reduce.19
  317.5 14.6 reduce-scatter.6
  335.1 31.8 reduce-scatter.8
  369.2 31.8 reduce-scatter.10
  404.0 26.1 reduce-scatter.4
  433.6 78.6 all-reduce.15
  514.9 67.9 all-reduce.17
